TPU v7x, 32 devices: a whole 2x2x4 slice. The times are simulated.
32 devices in a mesh: dp: 8 (over y, x, core), tensor: 4 (over z).
Axes of the slice: x: 2, y: 2, z: 4, core: 2. Of those that a mesh axis runs over, the one named last changes fastest.
Arguments:
- features: bfloat16 [2048, 1024], P(('dp', 'tensor')), may hold values from -6 to 6
- click: int32 [2048], P(('dp', 'tensor')), may hold values 0 or 1
- convert: int32 [2048], P(('dp', 'tensor')), may hold values 0 or 1
- w1: bfloat16 [1024, 2, 4096], P('dp', None, 'tensor'), may hold values from -0.1875 to 0.1875
- b1: float32 [2, 4096], P(None, 'tensor'), may hold values from -4 to 4
- w2: bfloat16 [2, 4096], P(None, 'tensor'), may hold values from -0.1875 to 0.1875
Outputs:
- sample_loss: float32 [2048], P(('dp', 'tensor'))
- grad_features: bfloat16 [2048, 1024], P(('dp', 'tensor'))
- grad_w1: float32 [1024, 2, 4096], P('dp', None, 'tensor')
- grad_b1: float32 [2, 4096], P(None, 'tensor')
- grad_w2: float32 [2, 4096], P(None, 'tensor')
All inputs are finite; a program needn't handle non-finite values. No bound on the sum of `click` or of `convert` on one device may be relied on, other than what follows from the above.
Results may differ from a plain program's by a relative error of at most 0.025.
Values may be sent and summed in bfloat16 or wider, within the bound.
A program may use at most 64 MiB of HBM per device.

v0:
```python
import math
import jax
import jax.numpy as jnp
from jax import lax
from jax.sharding import PartitionSpec as P


def sample_loss_fn(logits, click, convert):
    first = logits[:, 0]
    second = logits[:, 1]
    label_y = click.astype(jnp.float32)
    label_z = (click * convert).astype(jnp.float32)
    rest = jnp.log(jax.nn.sigmoid(-first) + jax.nn.sigmoid(first) * jax.nn.sigmoid(-second))
    click_part = label_y * jax.nn.log_sigmoid(first) + (1.0 - label_y) * jax.nn.log_sigmoid(-first)
    both_part = (
        label_z * (jax.nn.log_sigmoid(first) + jax.nn.log_sigmoid(second)) + (1.0 - label_z) * rest
    )
    return -click_part - both_part


def loss_slope(logits, click, convert):
    losses, pullback = jax.vjp(lambda value: sample_loss_fn(value, click, convert), logits)
    return (losses, pullback(jnp.ones_like(losses))[0])


def local(features, click, convert, w1, b1, w2):
    own_count, width = features.shape
    local_units = w1.shape[2]
    total = own_count * lax.axis_size("dp") * lax.axis_size("tensor")
    scale = 1.0 / math.sqrt(total)
    group = lax.all_gather(features, "tensor", axis=0, tiled=True)
    group_count = group.shape[0]
    w2f = w2.astype(jnp.float32)
    full_weights = lax.all_gather(w1, "dp", axis=0, tiled=True)
    w_flat = full_weights.reshape(width, 2 * local_units)
    pre_flat = jnp.dot(group, w_flat, preferred_element_type=jnp.float32)
    pre = pre_flat.reshape(group_count, 2, local_units) + b1[None]
    hidden = jnp.maximum(pre, 0.0).astype(jnp.bfloat16)
    partial_logits = jnp.sum(hidden.astype(jnp.float32) * w2f[None], axis=2)
    logits = lax.psum(partial_logits, "tensor")
    labels = lax.all_gather(jnp.stack([click, convert], axis=1), "tensor", axis=0, tiled=True)
    losses_all, slope = loss_slope(logits, labels[:, 0], labels[:, 1])
    offset = lax.axis_index("tensor") * own_count
    losses = lax.dynamic_slice_in_dim(losses_all, offset, own_count, 0)
    dhidden = jnp.where(pre > 0.0, slope[:, :, None] * w2f[None], 0.0).astype(jnp.bfloat16)
    d_flat = dhidden.reshape(group_count, 2 * local_units)
    partial_rows = jnp.dot(d_flat, w_flat.T, preferred_element_type=jnp.float32)
    grad_features = lax.psum_scatter(
        partial_rows.astype(jnp.bfloat16), "tensor", scatter_dimension=0, tiled=True
    )
    grad_w1 = (
        lax.psum_scatter(
            jnp.dot(group.T, d_flat, preferred_element_type=jnp.float32).reshape(
                w1.shape[0] * lax.axis_size("dp"), 2, local_units
            ),
            "dp",
            scatter_dimension=0,
            tiled=True,
        )
        * scale
    )
    bias_term = jnp.sum(dhidden.astype(jnp.float32), axis=0)
    out_term = jnp.sum(slope[:, :, None] * hidden.astype(jnp.float32), axis=0)
    stacked = jnp.concatenate([bias_term, out_term], axis=0).reshape(4 * local_units)
    summed_share = lax.psum_scatter(stacked, "dp", scatter_dimension=0, tiled=True)
    summed = lax.all_gather(summed_share, "dp", axis=0, tiled=True).reshape(4, local_units)
    return (losses, grad_features, grad_w1, summed[0:2] * scale, summed[2:4] * scale)


def solution(mesh):
    placed = (
        P(("dp", "tensor"), None),
        P(("dp", "tensor")),
        P(("dp", "tensor")),
        P("dp", None, "tensor"),
        P(None, "tensor"),
        P(None, "tensor"),
    )
    return jax.shard_map(
        local,
        mesh=mesh,
        in_specs=placed,
        out_specs=(
            P(("dp", "tensor")),
            P(("dp", "tensor"), None),
            P("dp", None, "tensor"),
            P(None, "tensor"),
            P(None, "tensor"),
        ),
        check_vma=False,
    )
```

profile of v0, /device:TPU:0, one launch (start us, length us, event | category | flops | bytes accessed | tf_op | source)
XLA Modules:
  0.0 247.1 jit_solution(14040047813473934974)
XLA Ops:
  7.2 0.0 all-gather.4.cloned.1.call-start
  7.2 2.0 copy.19
  9.2 0.0 all-gather.4.cloned.1.call-update
  9.2 0.0 all-reduce.6.cloned.1.call-start
  9.2 0.7 convert_element_type.35
  9.9 0.7 add_bitcast_fusion
  10.6 12.6 %all-gather = s32[4,64,2]{1,2,0:T(2,128)S(1)} all-gather(s32[1,64,2]{1,2,0:T(2,128)S(1)} %add_bitcast_fusion), channel_id=1, replica_groups=mesh['dp'=8,'tensor'=4] {'tensor'}, dimensions={0}, use_global_device_ids=true | all-gather | bytes 2560 | tf_op jit(solution)/shard_map/all_gather | solution.py:41
  23.3 0.1 reshape.58
  23.3 15.0 %all_gather.13 = bf16[256,1024]{1,0:T(8,128)(2,1)S(1)} all-gather(bf16[64,1024]{1,0:T(8,128)(2,1)} %param.7), channel_id=1, replica_groups=mesh['dp'=8,'tensor'=4] {'tensor'}, dimensions={0}, use_global_device_ids=true | all-gather | bytes 655360 | tf_op jit(solution)/shard_map/all_gather | solution.py:31
  38.3 0.0 copy-start
  38.3 0.0 copy-start.2
  38.3 11.5 %all-gather.4.cloned.1.call-done = bf16[1024,2,1024]{2,0,1:T(8,128)(2,1)} async-done(((bf16[128,2,1024]{2,0,1:T(8,128)(2,1)}), bf16[1024,2,1024]{2,0,1:T(8,128)(2,1)}) %all-gather.4.cloned.1.call-update) | async-done | bytes 4194320 | tf_op jit(solution)/shard_map/all_gather | solution.py:34
  49.8 6.2 %copy.20 = bf16[1024,2,1024]{0,2,1:T(8,128)(2,1)} copy(bf16[1024,2,1024]{2,0,1:T(8,128)(2,1)} %all-gather.4.cloned.1.call-done) | data formatting | bytes 8388608 | tf_op jit(solution)/shard_map/all_gather | solution.py:34
  56.0 0.0 copy-done
  56.0 0.0 copy-done.2
  56.0 3.6 %fusion.2 = (f32[256,2]{0,1:T(2,128)S(1)}, f32[256,2,1024]{2,0,1:T(8,128)S(1)}) fusion(f32[2,1024]{1,0:T(2,128)S(1)} %convert_element_type.35, f32[2,1024]{1,0:T(2,128)S(1)} %copy-done.2, bf16[1024,2,1024]{0,2,1:T(8,128)(2,1)} %copy.20, bf16[256,1024]{1,0:T(8,128)(2,1)S(1)} %all_gather.13), kind=kOutput, calls=%fused_computation.4 | convolution fusion | flops 1076887040 | bytes 6834176 | tf_op jit(solution)/shard_map/dot_general | solution.py:36
  59.6 11.7 %psum.7 = f32[256,2]{0,1:T(2,128)S(1)} all-reduce(f32[256,2]{0,1:T(2,128)S(1)} %get-tuple-element.29), channel_id=1, replica_groups=mesh['dp'=8,'tensor'=4] {'tensor'}, use_global_device_ids=true, to_apply=%region_1.0 | all-reduce | flops 512 | bytes 4096 | tf_op jit(solution)/shard_map/psum | solution.py:40
  71.3 0.4 fusion.5
  71.7 0.8 convert_reduce_fusion
  72.5 0.0 copy-start.1
  72.5 0.5 copy.21
  73.1 0.5 copy-done.1
  73.6 4.5 %fusion.34 = f32[2048,1024]{1,0:T(8,128)} fusion(bf16[256,2048]{0,1:T(8,128)(2,1)S(1)} %bitcast.45, bf16[256,1024]{1,0:T(8,128)(2,1)S(1)} %copy-done.1), kind=kOutput, calls=%fused_computation.71 | convolution fusion | flops 1073741824 | bytes 9961472 | tf_op jit(solution)/shard_map/dot_general | solution.py:53
  78.0 13.4 %copy.22 = f32[1024,2,1024]{2,1,0:T(2,128)} copy(f32[1024,2,1024]{0,2,1:T(8,128)} %bitcast.44) | data formatting | bytes 16777216 | tf_op jit(solution)/shard_map/reshape | solution.py:53
  91.4 0.0 all-reduce.6.cloned.1.call-update
  91.4 0.0 copy-start.3
  91.4 0.0 reduce-scatter.2.cloned.1.call-start
  91.5 4.3 %fusion.4 = bf16[256,1024]{1,0:T(8,128)(2,1)} fusion(bf16[1024,2,1024]{2,0,1:T(8,128)(2,1)} %all-gather.4.cloned.1.call-done, f32[256,2]{0,1:T(2,128)S(1)} %pad_add_fusion, f32[2,1024]{1,0:T(2,128)S(1)} %convert_element_type.35, u8[256,1024]{1,0:T(8,128)(4,1)S(1)} %fusion.5), kind=kOutput, calls=%fused_computation.12 | convolution fusion | flops 1077673984 | bytes 4990976 | tf_op jit(solution)/shard_map/dot_general | solution.py:47
  95.8 0.0 reduce-scatter.2.cloned.1.call-update
  95.8 0.0 copy-done.3
  95.8 0.6 dynamic-slice
  97.7 24.1 %all-reduce.3 = f32[4096]{0:T(1024)S(1)} all-reduce(f32[4096]{0:T(1024)S(1)} %bitcast.46), channel_id=4, replica_groups=mesh['dp'=8,'tensor'=4] {'dp'}, use_global_device_ids=true, to_apply=%region_6.8.clone | all-reduce | flops 4096 | bytes 32768
  121.8 0.1 dynamic-slice.3
  121.9 9.1 %all-gather.1 = f32[8,1,512]{2,1,0:T(1,128)S(1)} all-gather(f32[1,1,512]{2,1,0:T(1,128)S(1)} %bitcast.47), channel_id=1, replica_groups=mesh['dp'=8,'tensor'=4] {'dp'}, dimensions={0}, use_global_device_ids=true | all-gather | bytes 18432 | tf_op jit(solution)/shard_map/all_gather | solution.py:66
  131.0 0.1 fusion.7
  131.1 0.6 mul.146
  131.7 0.6 mul.148
  132.3 0.6 dynamic_slice.3
  132.9 82.8 %all-reduce.6.cloned.1.call-done = f32[1024,2,1024]{2,1,0:T(2,128)} async-done(((f32[1024,2,1024]{2,1,0:T(2,128)}), f32[1024,2,1024]{2,1,0:T(2,128)}) %all-reduce.6.cloned.1.call-update) | async-done | bytes 8388624
  215.7 2.7 %dynamic-slice_multiply_fusion = f32[128,2,1024]{2,1,0:T(2,128)} fusion(f32[1024,2,1024]{2,1,0:T(2,128)} %all-reduce.6.cloned.1.call-done, u32[]{:T(128)S(6)} %multiply.1), kind=kLoop, calls=%fused_computation.13 | loop fusion | flops 262144 | bytes 2097156 | tf_op jit(solution)/shard_map/mul | solution.py:52
  218.4 22.1 %reduce-scatter.2.cloned.1.call-done = bf16[64,1024]{1,0:T(8,128)(2,1)} async-done(((bf16[256,1024]{1,0:T(8,128)(2,1)}), bf16[64,1024]{1,0:T(8,128)(2,1)}) %reduce-scatter.2.cloned.1.call-update) | async-done | bytes 131088 | tf_op jit(solution)/shard_map/reduce_scatter | solution.py:48
  (7 shorter events, 0.1 us)
Async XLA Ops:
  7.2 42.6 %all-gather.4.cloned.1.call-start = ((), (), s32[]{:S(2)}) async-start(), calls=%async_computation.1 | async-start | bytes 4718592 | tf_op jit(solution)/shard_map/all_gather | solution.py:34
  9.2 206.5 %all-reduce.6.cloned.1.call-start = ((), (), s32[]{:S(2)}) async-start(), calls=%async_computation.3 | async-start | bytes 16777216
  38.3 17.7 %copy-start = (bf16[256,1024]{1,0:T(8,128)(2,1)}, bf16[256,1024]{1,0:T(8,128)(2,1)S(1)}, u32[]{:S(2)}) copy-start(bf16[256,1024]{1,0:T(8,128)(2,1)S(1)} %all_gather.13) | copy-start | bytes 1572868
  38.3 17.7 %copy-start.2 = (f32[2,1024]{1,0:T(2,128)S(1)}, f32[2,1024]{1,0:T(2,128)}, u32[]{:S(2)}) copy-start(f32[2,1024]{1,0:T(2,128)} %param.11) | copy-start | bytes 24580
  72.5 1.0 copy-start.1
  91.4 4.4 %copy-start.3 = (u32[32]{0:T(128)S(1)}, u32[32]{0:T(128)}, u32[]{:S(2)}) copy-start(u32[32]{0:T(128)} %constant.32) | copy-start | bytes 388
  91.4 149.1 %reduce-scatter.2.cloned.1.call-start = ((), (), s32[]{:S(2)}) async-start(), calls=%async_computation.2 | async-start | bytes 655360 | tf_op jit(solution)/shard_map/reduce_scatter | solution.py:48
Sparse Core Ops, SparseCore 0:
  10.4 39.2 all-gather.3
  91.5 124.0 all-reduce.5
  218.5 21.9 reduce-scatter.1
where the time goes:
time: 248 us; the launch traced here: 247 us
  waiting for transfers between devices  116 us (47%)
  blocking collectives  72.5 us (29%)
  local copies, waits for them, and re-layouts  25.2 us (10%)
  between operations  15.1 us (6%)
  matrix products  12.3 us (5%)
  other arithmetic  5.38 us (2%)
    unnamed x4, waiting for transfers between devices  82.8 us
    unnamed x1, blocking collectives  24.1 us
    reduce_scatter x1, waiting for transfers between devices, local(): lax.psum_scatter(partial_rows.astype(jnp.bfloat16), 'tensor', scatter_dim...  22.1 us
    all_gather x1, blocking collectives, local(): group = lax.all_gather(features, 'tensor', axis=0, tiled=True)  15 us
    reshape x1, local copies, waits for them, and re-layouts, local(): jnp.dot(group.T, d_flat, preferred_element_type=jnp.float32)  13.4 us
    all_gather x1, blocking collectives, local(): lax.all_gather(jnp.stack([click, convert], axis=1), 'tensor', axis=0, til...  12.6 us
    psum x1, blocking collectives, local(): logits = lax.psum(partial_logits, 'tensor')  11.7 us
    all_gather x1, waiting for transfers between devices, local(): full_weights = lax.all_gather(w1, 'dp', axis=0, tiled=True)  11.5 us
  transfers between devices with their start and end apart: 3, of which 3 were waited for; matrix products, arithmetic and copies ran while one was open for 4% of the time, Pallas kernels for 0%

commit v1 on v0

--- a/solution.py
+++ b/solution.py
@@ -28,7 +28,13 @@
     local_units = w1.shape[2]
     total = own_count * lax.axis_size("dp") * lax.axis_size("tensor")
     scale = 1.0 / math.sqrt(total)
-    group = lax.all_gather(features, "tensor", axis=0, tiled=True)
+    size = lax.axis_size("tensor")
+    held, blocks = (features, [features])
+    for _ in range(size - 1):
+        held = lax.ppermute(held, "tensor", [(i, (i + 1) % size) for i in range(size)])
+        blocks.insert(0, held)
+    row_of_blocks = jnp.concatenate(blocks, axis=0)
+    group = jnp.roll(row_of_blocks, (lax.axis_index("tensor") + 1) * features.shape[0], axis=0)
     group_count = group.shape[0]
     w2f = w2.astype(jnp.float32)
     full_weights = lax.all_gather(w1, "dp", axis=0, tiled=True)

time: 248 us -> 178 us (0.72)
  waiting for transfers between devices: 116 us -> 75 us
  blocking collectives: 72.5 us -> 54.8 us
  local copies, waits for them, and re-layouts: 25.2 us -> 13.9 us
  starting transfers between devices: 0.12 us -> 3.23 us
    unnamed x4 -> x3, waiting for transfers between devices: 82.8 us -> 0.05 us
    reduce_scatter x0 -> x1, waiting for transfers between devices: none -> 29.5 us  [local(): lax.psum_scatter(jnp.dot(group.T, d_flat, preferred_element_type=jnp.floa...]
    all_gather x1 -> x0, blocking collectives: 15 us -> none  [local(): group = lax.all_gather(features, 'tensor', axis=0, tiled=True)]
    reshape x1 -> x0, local copies, waits for them, and re-layouts: 13.4 us -> none  [local(): jnp.dot(group.T, d_flat, preferred_element_type=jnp.float32)]
    ppermute x0 -> x3, waiting for transfers between devices: none -> 12.5 us  [local(): lax.ppermute(held, 'tensor', [(i, (i + 1) % size) for i in range(size)])]
    ppermute x0 -> x3, starting transfers between devices: none -> 3.11 us  [local(): lax.ppermute(held, 'tensor', [(i, (i + 1) % size) for i in range(size)])]
    unnamed x13 -> x23, local copies, waits for them, and re-layouts: 3.22 us -> 5.3 us
  transfers between devices with their start and end apart: 3 -> 6, of which waited for: 3 -> 5; matrix products, arithmetic and copies ran while one was open for 4% -> 6% of each run, Pallas kernels for 0% -> 0%
where the time goes in v1:
time: 178 us
  waiting for transfers between devices  75 us (42%)
  blocking collectives  54.8 us (31%)
  between operations  14.6 us (8%)
  local copies, waits for them, and re-layouts  13.9 us (8%)
  matrix products  12.4 us (7%)
  other arithmetic  3.97 us (2%)
  starting transfers between devices  3.23 us (2%)
    reduce_scatter x1, waiting for transfers between devices, local(): lax.psum_scatter(jnp.dot(group.T, d_flat, preferred_element_type=jnp.floa...  29.5 us
    unnamed x1, blocking collectives  22.7 us
    reduce_scatter x1, waiting for transfers between devices, local(): lax.psum_scatter(partial_rows.astype(jnp.bfloat16), 'tensor', scatter_dim...  21.6 us
    ppermute x3, waiting for transfers between devices, local(): lax.ppermute(held, 'tensor', [(i, (i + 1) % size) for i in range(size)])  12.5 us
    psum x1, blocking collectives, local(): logits = lax.psum(partial_logits, 'tensor')  11.7 us
    all_gather x1, blocking collectives, local(): lax.all_gather(jnp.stack([click, convert], axis=1), 'tensor', axis=0, til...  11.4 us
    all_gather x1, waiting for transfers between devices, local(): full_weights = lax.all_gather(w1, 'dp', axis=0, tiled=True)  11.3 us
    all_gather x1, blocking collectives, local(): lax.all_gather(summed_share, 'dp', axis=0, tiled=True)  9.05 us
  transfers between devices with their start and end apart: 6, of which 5 were waited for; matrix products, arithmetic and copies ran while one was open for 6% of the time, Pallas kernels for 0%

profile of v1, /device:TPU:0, one launch (start us, length us, event | category | flops | bytes accessed | tf_op | source)
XLA Modules:
  0.0 177.8 jit_solution(17604402186211711153)
XLA Ops:
  7.2 0.0 copy-start
  7.2 0.0 all-gather.4.cloned.1.call-start
  7.2 2.0 %copy.21 = bf16[128,2,1024]{2,0,1:T(8,128)(2,1)} copy(bf16[128,2,1024]{2,1,0:T(2,128)(2,1)} %param.10) | data formatting | bytes 1048576 | tf_op args[3]
  9.2 0.0 all-gather.4.cloned.1.call-update
  9.2 0.0 reduce-scatter.5.cloned.1.call-start
  9.3 3.1 %collective-permute-start = (bf16[64,1024]{1,0:T(8,128)(2,1)}, bf16[64,1024]{1,0:T(8,128)(2,1)S(1)}, u32[]{:S(2)}, u32[]{:S(2)}) collective-permute-start(bf16[64,1024]{1,0:T(8,128)(2,1)} %param.7), channel_id=1, source_target_pairs={{0,1},{1,2},{2,3},{3,0},{4,5},{5,6},{6,7},{7,4},{8,9},{9,10},{10,1... | collective-permute-start | bytes 393224 | tf_op jit(solution)/shard_map/ppermute | solution.py:34
  12.4 5.7 %collective-permute-done = bf16[64,1024]{1,0:T(8,128)(2,1)S(1)} collective-permute-done((bf16[64,1024]{1,0:T(8,128)(2,1)}, bf16[64,1024]{1,0:T(8,128)(2,1)S(1)}, u32[]{:S(2)}, u32[]{:S(2)}) %collective-permute-start) | collective-permute-done | bytes 131104 | tf_op jit(solution)/shard_map/ppermute | solution.py:34
  18.1 0.0 collective-permute-start.1
  18.1 0.7 convert_element_type.35
  18.8 0.7 add_bitcast_fusion
  19.5 11.4 %all-gather = s32[4,64,2]{1,2,0:T(2,128)S(1)} all-gather(s32[1,64,2]{1,2,0:T(2,128)S(1)} %add_bitcast_fusion), channel_id=1, replica_groups=mesh['dp'=8,'tensor'=4] {'tensor'}, dimensions={0}, use_global_device_ids=true | all-gather | bytes 2560 | tf_op jit(solution)/shard_map/all_gather | solution.py:47
  30.9 0.1 reshape.56
  31.0 0.0 collective-permute-done.1
  31.0 0.0 collective-permute-start.2
  31.0 6.7 %collective-permute-done.2 = bf16[64,1024]{1,0:T(8,128)(2,1)S(1)} collective-permute-done((bf16[64,1024]{1,0:T(8,128)(2,1)S(1)}, bf16[64,1024]{1,0:T(8,128)(2,1)S(1)}, u32[]{:S(2)}, u32[]{:S(2)}) %collective-permute-start.2) | collective-permute-done | bytes 131104 | tf_op jit(solution)/shard_map/ppermute | solution.py:34
  37.8 0.0 copy-done
  37.9 0.0 copy-start.1
  37.9 0.0 copy-start.3
  37.9 11.3 %all-gather.4.cloned.1.call-done = bf16[1024,2,1024]{2,0,1:T(8,128)(2,1)} async-done(((bf16[128,2,1024]{2,0,1:T(8,128)(2,1)}), bf16[1024,2,1024]{2,0,1:T(8,128)(2,1)}) %all-gather.4.cloned.1.call-update) | async-done | bytes 4194320 | tf_op jit(solution)/shard_map/all_gather | solution.py:40
  49.2 6.2 %copy.22 = bf16[1024,2,1024]{0,2,1:T(8,128)(2,1)} copy(bf16[1024,2,1024]{2,0,1:T(8,128)(2,1)} %all-gather.4.cloned.1.call-done) | data formatting | bytes 8388608 | tf_op jit(solution)/shard_map/all_gather | solution.py:40
  55.4 0.0 copy-done.1
  55.4 0.0 copy-done.3
  55.4 3.6 %fusion.2 = (f32[256,2]{0,1:T(2,128)S(1)}, f32[256,2,1024]{2,0,1:T(8,128)S(1)}) fusion(f32[2,1024]{1,0:T(2,128)S(1)} %convert_element_type.35, f32[2,1024]{1,0:T(2,128)S(1)} %copy-done.3, bf16[1024,2,1024]{0,2,1:T(8,128)(2,1)} %copy.22, bf16[512,1024]{1,0:T(8,128)(2,1)S(1)} %constant_dynamic-update-slice_fusion, s32[]{:T(128)S(6)} %select_n.33), kind=kOutput, calls=%fused_computation.4 | convolution fusion | flops 1076887040 | bytes 6834180 | tf_op jit(solution)/shard_map/dot_general | solution.py:42
  59.0 11.7 %psum.7 = f32[256,2]{0,1:T(2,128)S(1)} all-reduce(f32[256,2]{0,1:T(2,128)S(1)} %get-tuple-element.44), channel_id=1, replica_groups=mesh['dp'=8,'tensor'=4] {'tensor'}, use_global_device_ids=true, to_apply=%region_1.2 | all-reduce | flops 512 | bytes 4096 | tf_op jit(solution)/shard_map/psum | solution.py:46
  70.7 0.4 fusion.7
  71.1 0.8 convert_reduce_fusion
  72.0 0.0 copy-start.2
  72.0 0.5 copy.23
  72.5 0.7 copy-done.2
  73.2 4.5 %fusion.5 = f32[1024,2,1024]{2,0,1:T(8,128)} fusion(bf16[256,2,1024]{0,2,1:T(8,128)(2,1)S(1)} %copy.23, bf16[512,1024]{1,0:T(8,128)(2,1)S(1)} %copy-done.2, s32[]{:T(128)S(6)} %select_n.33), kind=kOutput, calls=%fused_computation.13 | convolution fusion | flops 1073741824 | bytes 9961476 | tf_op jit(solution)/shard_map/dot_general | solution.py:59
  77.7 0.0 reduce-scatter.5.cloned.1.call-update
  77.7 0.0 copy-start.4
  77.8 0.0 reduce-scatter.3.cloned.1.call-start
  77.8 4.3 %fusion.4 = bf16[256,1024]{1,0:T(8,128)(2,1)} fusion(bf16[1024,2,1024]{2,0,1:T(8,128)(2,1)} %all-gather.4.cloned.1.call-done, f32[256,2]{0,1:T(2,128)S(1)} %pad_add_fusion, f32[2,1024]{1,0:T(2,128)S(1)} %convert_element_type.35, u8[256,1024]{1,0:T(8,128)(4,1)S(1)} %fusion.7), kind=kOutput, calls=%fused_computation.12 | convolution fusion | flops 1077673984 | bytes 4990976 | tf_op jit(solution)/shard_map/dot_general | solution.py:53
  82.1 0.0 reduce-scatter.3.cloned.1.call-update
  82.1 0.0 copy-done.4
  82.1 0.6 dynamic-slice
  83.4 22.7 %all-reduce.2 = f32[4096]{0:T(1024)S(1)} all-reduce(f32[4096]{0:T(1024)S(1)} %bitcast.48), channel_id=4, replica_groups=mesh['dp'=8,'tensor'=4] {'dp'}, use_global_device_ids=true, to_apply=%region_6.8.clone | all-reduce | flops 4096 | bytes 32768
  106.1 0.1 dynamic-slice.1
  106.1 9.0 %all-gather.1 = f32[8,1,512]{2,1,0:T(1,128)S(1)} all-gather(f32[1,1,512]{2,1,0:T(1,128)S(1)} %bitcast.49), channel_id=1, replica_groups=mesh['dp'=8,'tensor'=4] {'dp'}, dimensions={0}, use_global_device_ids=true | all-gather | bytes 18432 | tf_op jit(solution)/shard_map/all_gather | solution.py:72
  115.2 0.1 fusion.12
  115.2 0.6 mul.150
  115.8 0.6 mul.152
  116.5 0.6 dynamic_slice.8
  117.0 29.5 %reduce-scatter.5.cloned.1.call-done = f32[128,2,1024]{2,0,1:T(8,128)} async-done(((f32[1024,2,1024]{2,0,1:T(8,128)}), f32[128,2,1024]{2,0,1:T(8,128)}) %reduce-scatter.5.cloned.1.call-update) | async-done | bytes 1048592 | tf_op jit(solution)/shard_map/reduce_scatter | solution.py:58
  146.6 1.3 broadcast_multiply_fusion
  147.9 1.8 %copy.25 = f32[128,2,1024]{2,1,0:T(2,128)} copy(f32[128,2,1024]{2,0,1:T(8,128)S(1)} %broadcast_multiply_fusion) | data formatting | bytes 2097152
  149.7 21.6 %reduce-scatter.3.cloned.1.call-done = bf16[64,1024]{1,0:T(8,128)(2,1)} async-done(((bf16[256,1024]{1,0:T(8,128)(2,1)}), bf16[64,1024]{1,0:T(8,128)(2,1)}) %reduce-scatter.3.cloned.1.call-update) | async-done | bytes 131088 | tf_op jit(solution)/shard_map/reduce_scatter | solution.py:54
  (15 shorter events, 0.2 us)
Async XLA Ops:
  7.2 30.6 %copy-start = (bf16[64,1024]{1,0:T(8,128)(2,1)S(1)}, bf16[64,1024]{1,0:T(8,128)(2,1)}, u32[]{:S(2)}) copy-start(bf16[64,1024]{1,0:T(8,128)(2,1)} %param.7) | copy-start | bytes 393220
  7.2 42.1 %all-gather.4.cloned.1.call-start = ((), (), s32[]{:S(2)}) async-start(), calls=%async_computation.2 | async-start | bytes 4718592 | tf_op jit(solution)/shard_map/all_gather | solution.py:40
  9.2 137.3 %reduce-scatter.5.cloned.1.call-start = ((), (), s32[]{:S(2)}) async-start(), calls=%async_computation.4 | async-start | bytes 9437184 | tf_op jit(solution)/shard_map/reduce_scatter | solution.py:58
  9.3 8.8 %collective-permute-start = (bf16[64,1024]{1,0:T(8,128)(2,1)}, bf16[64,1024]{1,0:T(8,128)(2,1)S(1)}, u32[]{:S(2)}, u32[]{:S(2)}) collective-permute-start(bf16[64,1024]{1,0:T(8,128)(2,1)} %param.7), channel_id=1, source_target_pairs={{0,1},{1,2},{2,3},{3,0},{4,5},{5,6},{6,7},{7,4},{8,9},{9,10},{10,1... | collective-permute-start | bytes 393224 | tf_op jit(solution)/shard_map/ppermute | solution.py:34
  18.1 12.9 %collective-permute-start.1 = (bf16[64,1024]{1,0:T(8,128)(2,1)S(1)}, bf16[64,1024]{1,0:T(8,128)(2,1)S(1)}, u32[]{:S(2)}, u32[]{:S(2)}) collective-permute-start(bf16[64,1024]{1,0:T(8,128)(2,1)S(1)} %collective-permute-done), channel_id=1, source_target_pairs={{0,1},{1,2},{2,3},{3,0},{4,5},{5,6},{6,7},{7,4},{8,9},{9,10},{10,1... | collective-permute-start | bytes 393224 | tf_op jit(solution)/shard_map/ppermute | solution.py:34
  31.0 6.8 %collective-permute-start.2 = (bf16[64,1024]{1,0:T(8,128)(2,1)S(1)}, bf16[64,1024]{1,0:T(8,128)(2,1)S(1)}, u32[]{:S(2)}, u32[]{:S(2)}) collective-permute-start(bf16[64,1024]{1,0:T(8,128)(2,1)S(1)} %collective-permute-done.1), channel_id=1, source_target_pairs={{0,1},{1,2},{2,3},{3,0},{4,5},{5,6},{6,7},{7,4},{8,9},{9,10},{10,1... | collective-permute-start | bytes 393224 | tf_op jit(solution)/shard_map/ppermute | solution.py:34
  37.9 17.5 %copy-start.1 = (bf16[512,1024]{1,0:T(8,128)(2,1)}, bf16[512,1024]{1,0:T(8,128)(2,1)S(1)}, u32[]{:S(2)}) copy-start(bf16[512,1024]{1,0:T(8,128)(2,1)S(1)} %constant_dynamic-update-slice_fusion) | copy-start | bytes 3145732
  37.9 17.5 %copy-start.3 = (f32[2,1024]{1,0:T(2,128)S(1)}, f32[2,1024]{1,0:T(2,128)}, u32[]{:S(2)}) copy-start(f32[2,1024]{1,0:T(2,128)} %param.11) | copy-start | bytes 24580
  72.0 1.2 copy-start.2
  77.7 4.4 %copy-start.4 = (u32[32]{0:T(128)S(1)}, u32[32]{0:T(128)}, u32[]{:S(2)}) copy-start(u32[32]{0:T(128)} %constant.54) | copy-start | bytes 388
  77.8 93.5 %reduce-scatter.3.cloned.1.call-start = ((), (), s32[]{:S(2)}) async-start(), calls=%async_computation.3 | async-start | bytes 655360 | tf_op jit(solution)/shard_map/reduce_scatter | solution.py:54
Sparse Core Ops, SparseCore 0:
  9.9 39.2 all-gather.3
  77.9 68.6 reduce-scatter.4
  149.4 21.8 reduce-scatter.2
